TPU v7x, 256 devices: a whole 4x4x8 slice. The times are simulated.
256 devices in a mesh: pair: 32 (over x, z_hi, core), aux: 8 (over z_lo, y).
Axes of the slice: x: 4, y: 4, z: 8 (z_hi: 4, z_lo: 2; z = z_hi * 2 + z_lo), core: 2. Of those that a mesh axis runs over, the one named last changes fastest.
Arguments:
- integrals: float32 [32, 640, 4096], P(None, 'aux', 'pair'), may hold values from -6 to 6
- factor: float32 [4096, 4096], P('aux', 'pair'), may hold values from -1 to 2, as said below
- diag_inverse: float32 [8, 512, 512], P('aux'), may hold values from -1 to 1, as said below
Outputs:
- transformed: float32 [32, 640, 4096], P('pair', None, 'aux')
Inputs may be any that keep to these rules, and one draw needn't show every extreme that they name: factor is zero above its diagonal. diag_inverse[j] is the inverse, up to rounding, of the factor's j-th diagonal block of 512 x 512.
All inputs are finite; a program needn't handle non-finite values.
Results may differ from a plain program's by a relative error of at most 0.0001.
Values sent between devices are 32-bit elements; how exact they have to be, the bound alone decides.
No kernel may reach another device: no remote copies, remote signals or barrier semaphores. Data moves between devices by JAX's collectives and lax.ppermute only.
A program may use at most 128 MiB of HBM per device.

v0:
```python
import jax
import jax.numpy as jnp
from jax import lax
from jax.sharding import PartitionSpec as P


def from_root(x, axis, root):
    mine = lax.axis_index(axis) == root
    return lax.psum(jnp.where(mine, x, jnp.zeros_like(x)), axis)


def product(left, right):
    return jnp.dot(left, right, precision=lax.Precision.HIGHEST, preferred_element_type=jnp.float32)


def local(integrals, factor, diag_inverse):
    relaid = lax.all_to_all(
        lax.all_to_all(integrals, "pair", split_axis=0, concat_axis=2, tiled=True),
        "aux",
        split_axis=2,
        concat_axis=1,
        tiled=True,
    )
    occ_count, virt_count, panel_width = relaid.shape
    remain = relaid.reshape(occ_count * virt_count, panel_width)
    row_panel = lax.all_gather(factor, "pair", axis=1, tiled=True)
    inverse_t = diag_inverse[0].T
    own_index = lax.axis_index("aux")
    panel_count = lax.axis_size("aux")
    result = jnp.zeros_like(remain)
    for step in range(panel_count):
        result = lax.cond(own_index == step, lambda: product(remain, inverse_t), lambda: result)
        if step + 1 < panel_count:
            factor_block = row_panel[:, step * panel_width : (step + 1) * panel_width].T
            arrived = from_root(result, "aux", step)
            remain = lax.cond(
                own_index > step, lambda: remain - product(arrived, factor_block), lambda: remain
            )
    return result.reshape(occ_count, virt_count, panel_width)


def solution(mesh):
    in_specs = (P(None, "aux", "pair"), P("aux", "pair"), P("aux", None, None))
    out_specs = P("pair", None, "aux")
    return jax.shard_map(local, mesh=mesh, in_specs=in_specs, out_specs=out_specs, check_vma=False)
```

profile of v0, /device:TPU:56, one launch (start us, length us, event | category | flops | bytes accessed | tf_op | source)
XLA Modules:
  0.0 783.9 jit_solution(10869943194843136534)
XLA Ops:
  7.4 1.8 copy.26
  9.2 53.9 %all_to_all.33 = f32[32,80,128]{2,1,0:T(8,128)S(1)} all-to-all(f32[32,80,128]{2,1,0:T(8,128)} %param.33), channel_id=1, replica_groups=mesh['pair'=32,'aux'=8] {'pair'}, dimensions={0} | all-to-all | bytes 2621440 | tf_op jit(solution)/shard_map/all_to_all | solution.py:18
  63.5 5.1 copy.22
  68.7 5.7 all-to-all-start.1
  74.7 52.9 %all-to-all-done.1 = f32[1,80,4096]{1,0,2:T(1,128)} async-done(((f32[1,80,4096]{1,0,2:T(1,128)}), f32[1,80,4096]{1,0,2:T(1,128)}, u32[]{:S(2)}, u32[]{:S(2)}) %all-to-all-start.1) | async-done | bytes 1310752 | tf_op jit(solution)/shard_map/all_to_all | solution.py:17
  127.6 2.8 copy.27
  130.4 2.1 copy.24
  132.5 1.2 conditional.15
  135.0 6.2 slice_bitcast_fusion
  141.2 77.3 %all-reduce.8.cloned.1.call-done = f32[640,512]{1,0:T(8,128)} async-done(((f32[640,512]{1,0:T(8,128)}), f32[640,512]{1,0:T(8,128)}) %all-reduce.8.cloned.1.call-update) | async-done | bytes 1310736 | tf_op jit(solution)/shard_map/psum | solution.py:9
  218.5 4.0 conditional.16
  218.5 4.0 convolution_subtract_fusion
  223.8 85.2 %all-reduce.10.cloned.1.call-done = f32[640,512]{1,0:T(8,128)} async-done(((f32[640,512]{1,0:T(8,128)}), f32[640,512]{1,0:T(8,128)}) %all-reduce.10.cloned.1.call-update) | async-done | bytes 1310736 | tf_op jit(solution)/shard_map/psum | solution.py:9
  309.0 4.5 conditional.18
  309.5 4.0 convolution_subtract_fusion.1
  314.8 87.7 %all-reduce.12.cloned.1.call-done = f32[640,512]{1,0:T(8,128)} async-done(((f32[640,512]{1,0:T(8,128)}), f32[640,512]{1,0:T(8,128)}) %all-reduce.12.cloned.1.call-update) | async-done | bytes 1310736 | tf_op jit(solution)/shard_map/psum | solution.py:9
  402.5 4.0 conditional.20
  402.5 4.0 convolution_subtract_fusion.2
  407.8 87.0 %all-reduce.14.cloned.1.call-done = f32[640,512]{1,0:T(8,128)} async-done(((f32[640,512]{1,0:T(8,128)}), f32[640,512]{1,0:T(8,128)}) %all-reduce.14.cloned.1.call-update) | async-done | bytes 1310736 | tf_op jit(solution)/shard_map/psum | solution.py:9
  494.8 4.0 conditional.22
  494.8 4.0 convolution_subtract_fusion.3
  500.3 86.1 %all-reduce.16.cloned.1.call-done = f32[640,512]{1,0:T(8,128)} async-done(((f32[640,512]{1,0:T(8,128)}), f32[640,512]{1,0:T(8,128)}) %all-reduce.16.cloned.1.call-update) | async-done | bytes 1310736 | tf_op jit(solution)/shard_map/psum | solution.py:9
  586.4 4.0 conditional.24
  586.4 4.0 convolution_subtract_fusion.4
  591.7 85.0 %all-reduce.18.cloned.1.call-done = f32[640,512]{1,0:T(8,128)} async-done(((f32[640,512]{1,0:T(8,128)}), f32[640,512]{1,0:T(8,128)}) %all-reduce.18.cloned.1.call-update) | async-done | bytes 1310736 | tf_op jit(solution)/shard_map/psum | solution.py:9
  676.7 4.0 conditional.26
  676.7 4.0 convolution_subtract_fusion.5
  682.0 87.0 %all-reduce.20.cloned.1.call-done = f32[640,512]{1,0:T(8,128)} async-done(((f32[640,512]{1,0:T(8,128)}), f32[640,512]{1,0:T(8,128)}) %all-reduce.20.cloned.1.call-update) | async-done | bytes 1310736 | tf_op jit(solution)/shard_map/psum | solution.py:9
  768.9 3.9 conditional.28
  769.1 3.7 convolution_subtract_fusion.6
  772.9 3.3 conditional.29
  772.9 3.3 convolution_bitcast_fusion
  (35 shorter events, 11.0 us)
Async XLA Ops:
  7.4 127.7 %all-gather.2.cloned.1.call-start = ((), (), s32[]{:S(2)}) async-start(), calls=%async_computation.3 | async-start | bytes 8650752 | tf_op jit(solution)/shard_map/all_gather | solution.py:26
  68.7 5.7 copy-start
  68.7 59.0 %all-to-all-start.1 = ((f32[1,80,4096]{1,0,2:T(1,128)}), f32[1,80,4096]{1,0,2:T(1,128)}, u32[]{:S(2)}, u32[]{:S(2)}) async-start(f32[1,80,4096]{1,0,2:T(1,128)} %copy.22), calls=%async_computation.1 | async-start | bytes 4194304 | tf_op jit(solution)/shard_map/all_to_all | solution.py:17
  74.4 144.1 %all-reduce.8.cloned.1.call-start = ((), (), s32[]{:S(2)}) async-start(), calls=%async_computation.2 | async-start | bytes 2621440 | tf_op jit(solution)/shard_map/psum | solution.py:9
  135.0 174.1 %all-reduce.10.cloned.1.call-start = ((), (), s32[]{:S(2)}) async-start(), calls=%async_computation.4 | async-start | bytes 2621440 | tf_op jit(solution)/shard_map/psum | solution.py:9
  223.7 178.7 %all-reduce.12.cloned.1.call-start = ((), (), s32[]{:S(2)}) async-start(), calls=%async_computation.5 | async-start | bytes 2621440 | tf_op jit(solution)/shard_map/psum | solution.py:9
  314.7 180.1 %all-reduce.14.cloned.1.call-start = ((), (), s32[]{:S(2)}) async-start(), calls=%async_computation.6 | async-start | bytes 2621440 | tf_op jit(solution)/shard_map/psum | solution.py:9
  407.8 178.6 %all-reduce.16.cloned.1.call-start = ((), (), s32[]{:S(2)}) async-start(), calls=%async_computation.7 | async-start | bytes 2621440 | tf_op jit(solution)/shard_map/psum | solution.py:9
  500.3 176.4 %all-reduce.18.cloned.1.call-start = ((), (), s32[]{:S(2)}) async-start(), calls=%async_computation.8 | async-start | bytes 2621440 | tf_op jit(solution)/shard_map/psum | solution.py:9
  591.7 177.3 %all-reduce.20.cloned.1.call-start = ((), (), s32[]{:S(2)}) async-start(), calls=%async_computation.9 | async-start | bytes 2621440 | tf_op jit(solution)/shard_map/psum | solution.py:9
Sparse Core Ops, SparseCore 0:
  10.7 112.6 all-gather.1
Sparse Core Ops, SparseCore 1:
  135.0 83.4 all-reduce.7
  223.8 85.1 all-reduce.9
  314.8 87.6 all-reduce.11
  407.8 86.9 all-reduce.13
  500.4 86.0 all-reduce.15
  591.8 84.9 all-reduce.17
  682.1 86.8 all-reduce.19
where the time goes:
time: 792 us; the launch traced here: 784 us
  waiting for transfers between devices  648 us (82%)
  blocking collectives  53.9 us (7%)
  matrix products  31.2 us (4%)
  local copies, waits for them, and re-layouts  19.9 us (3%)
  between operations  15.3 us (2%)
  other arithmetic  8.41 us (1%)
    psum x7, waiting for transfers between devices, from_root(): return lax.psum(jnp.where(mine, x, jnp.zeros_like(x)), axis)  595 us
    all_to_all x1, blocking collectives, local(): lax.all_to_all(integrals, 'pair', split_axis=0, concat_axis=2, tiled=True)  53.9 us
    all_to_all x1, waiting for transfers between devices, local(): lax.all_to_all(lax.all_to_all(integrals, 'pair', split_axis=0, concat_axi...  52.9 us
    dot_general x8, matrix products, product(): jnp.dot(left, right, precision=lax.Precision.HIGHEST, preferred_element_t...  31.2 us
  transfers between devices with their start and end apart: 9, of which 8 were waited for; matrix products, arithmetic and copies ran while one was open for 2% of the time, Pallas kernels for 0%

commit v1 on v0

--- a/solution.py
+++ b/solution.py
@@ -2,6 +2,12 @@
 import jax.numpy as jnp
 from jax import lax
 from jax.sharding import PartitionSpec as P
+
+
+def swap_blocks(x, axis, split, join):
+    pieces = jnp.split(x, lax.axis_size(axis), axis=split)
+    arrived = lax.all_to_all(jnp.stack(pieces), axis, 0, 0)
+    return jnp.concatenate(arrived, axis=join)
 
 
 def from_root(x, axis, root):
@@ -14,12 +20,8 @@
 
 
 def local(integrals, factor, diag_inverse):
-    relaid = lax.all_to_all(
-        lax.all_to_all(integrals, "pair", split_axis=0, concat_axis=2, tiled=True),
-        "aux",
-        split_axis=2,
-        concat_axis=1,
-        tiled=True,
+    relaid = swap_blocks(
+        lax.all_to_all(integrals, "pair", split_axis=0, concat_axis=2, tiled=True), "aux", 2, 1
     )
     occ_count, virt_count, panel_width = relaid.shape
     remain = relaid.reshape(occ_count * virt_count, panel_width)

time: 792 us -> 776 us (0.980)
  waiting for transfers between devices: 648 us -> 637 us
    all_to_all x1, waiting for transfers between devices: 52.9 us -> 44.6 us  [swap_blocks(): arrived = lax.all_to_all(jnp.stack(pieces), axis, 0, 0)]
  transfers between devices with their start and end apart: 9 -> 9, of which waited for: 8 -> 9; matrix products, arithmetic and copies ran while one was open for 2% -> 2% of each run, Pallas kernels for 0% -> 0%
where the time goes in v1:
time: 776 us; the launch traced here: 768 us
  waiting for transfers between devices  637 us (82%)
  blocking collectives  54.1 us (7%)
  matrix products  31.2 us (4%)
  between operations  15.3 us (2%)
  local copies, waits for them, and re-layouts  14.8 us (2%)
  other arithmetic  8.49 us (1%)
    psum x7, waiting for transfers between devices, from_root(): return lax.psum(jnp.where(mine, x, jnp.zeros_like(x)), axis)  591 us
    all_to_all x1, blocking collectives, local(): lax.all_to_all(integrals, 'pair', split_axis=0, concat_axis=2, tiled=True)  54.1 us
    all_to_all x1, waiting for transfers between devices, swap_blocks(): arrived = lax.all_to_all(jnp.stack(pieces), axis, 0, 0)  44.6 us
    dot_general x8, matrix products, product(): jnp.dot(left, right, precision=lax.Precision.HIGHEST, preferred_element_t...  31.2 us
  transfers between devices with their start and end apart: 9, of which 9 were waited for; matrix products, arithmetic and copies ran while one was open for 2% of the time, Pallas kernels for 0%

profile of v1, /device:TPU:56, one launch (start us, length us, event | category | flops | bytes accessed | tf_op | source)
XLA Modules:
  0.0 767.7 jit_solution(4415548865159199285)
XLA Ops:
  7.4 1.8 copy.25
  9.2 54.1 %all_to_all.23 = f32[32,80,128]{2,1,0:T(8,128)S(1)} all-to-all(f32[32,80,128]{2,1,0:T(8,128)} %param.33), channel_id=1, replica_groups=mesh['pair'=32,'aux'=8] {'pair'}, dimensions={0} | all-to-all | bytes 2621440 | tf_op jit(solution)/shard_map/all_to_all | solution.py:24
  64.8 2.0 stack.35
  66.8 1.8 copy.23
  68.6 5.5 all-to-all-start.1
  74.5 44.6 %all-to-all-done.1 = f32[8,1,80,512]{3,2,1,0:T(8,128)S(1)} async-done(((f32[8,1,80,512]{3,2,1,0:T(8,128)}), f32[8,1,80,512]{3,2,1,0:T(8,128)S(1)}, u32[]{:S(2)}, u32[]{:S(2)}) %all-to-all-start.1) | async-done | bytes 1310752 | tf_op jit(solution)/shard_map/all_to_all | solution.py:9
  119.1 1.2 conditional.15
  121.6 1.3 all-gather.2.cloned.1.call-done
  122.9 6.2 slice_bitcast_fusion
  129.1 73.1 %all-reduce.8.cloned.1.call-done = f32[640,512]{1,0:T(8,128)} async-done(((f32[640,512]{1,0:T(8,128)}), f32[640,512]{1,0:T(8,128)}) %all-reduce.8.cloned.1.call-update) | async-done | bytes 1310736 | tf_op jit(solution)/shard_map/psum | solution.py:15
  202.2 4.0 conditional.16
  202.2 4.0 convolution_subtract_fusion
  207.6 85.2 %all-reduce.10.cloned.1.call-done = f32[640,512]{1,0:T(8,128)} async-done(((f32[640,512]{1,0:T(8,128)}), f32[640,512]{1,0:T(8,128)}) %all-reduce.10.cloned.1.call-update) | async-done | bytes 1310736 | tf_op jit(solution)/shard_map/psum | solution.py:15
  292.8 4.5 conditional.18
  293.2 4.0 convolution_subtract_fusion.1
  298.6 87.7 %all-reduce.12.cloned.1.call-done = f32[640,512]{1,0:T(8,128)} async-done(((f32[640,512]{1,0:T(8,128)}), f32[640,512]{1,0:T(8,128)}) %all-reduce.12.cloned.1.call-update) | async-done | bytes 1310736 | tf_op jit(solution)/shard_map/psum | solution.py:15
  386.3 4.0 conditional.20
  386.3 4.0 convolution_subtract_fusion.2
  391.6 87.0 %all-reduce.14.cloned.1.call-done = f32[640,512]{1,0:T(8,128)} async-done(((f32[640,512]{1,0:T(8,128)}), f32[640,512]{1,0:T(8,128)}) %all-reduce.14.cloned.1.call-update) | async-done | bytes 1310736 | tf_op jit(solution)/shard_map/psum | solution.py:15
  478.6 4.0 conditional.22
  478.6 4.0 convolution_subtract_fusion.3
  484.1 86.0 %all-reduce.16.cloned.1.call-done = f32[640,512]{1,0:T(8,128)} async-done(((f32[640,512]{1,0:T(8,128)}), f32[640,512]{1,0:T(8,128)}) %all-reduce.16.cloned.1.call-update) | async-done | bytes 1310736 | tf_op jit(solution)/shard_map/psum | solution.py:15
  570.2 4.0 conditional.24
  570.2 4.0 convolution_subtract_fusion.4
  575.5 85.0 %all-reduce.18.cloned.1.call-done = f32[640,512]{1,0:T(8,128)} async-done(((f32[640,512]{1,0:T(8,128)}), f32[640,512]{1,0:T(8,128)}) %all-reduce.18.cloned.1.call-update) | async-done | bytes 1310736 | tf_op jit(solution)/shard_map/psum | solution.py:15
  660.5 4.0 conditional.26
  660.5 4.0 convolution_subtract_fusion.5
  665.8 86.9 %all-reduce.20.cloned.1.call-done = f32[640,512]{1,0:T(8,128)} async-done(((f32[640,512]{1,0:T(8,128)}), f32[640,512]{1,0:T(8,128)}) %all-reduce.20.cloned.1.call-update) | async-done | bytes 1310736 | tf_op jit(solution)/shard_map/psum | solution.py:15
  752.7 3.9 conditional.28
  752.9 3.7 convolution_subtract_fusion.6
  756.7 3.3 conditional.29
  756.7 3.3 convolution_bitcast_fusion
  (35 shorter events, 12.1 us)
Async XLA Ops:
  7.4 115.5 %all-gather.2.cloned.1.call-start = ((), (), s32[]{:S(2)}) async-start(), calls=%async_computation.3 | async-start | bytes 8650752 | tf_op jit(solution)/shard_map/all_gather | solution.py:28
  68.6 5.5 copy-start
  68.6 50.5 %all-to-all-start.1 = ((f32[8,1,80,512]{3,2,1,0:T(8,128)}), f32[8,1,80,512]{3,2,1,0:T(8,128)S(1)}, u32[]{:S(2)}, u32[]{:S(2)}) async-start(f32[8,1,80,512]{3,2,1,0:T(8,128)} %copy.23), calls=%async_computation.1 | async-start | bytes 2621440 | tf_op jit(solution)/shard_map/all_to_all | solution.py:9
  74.2 128.1 %all-reduce.8.cloned.1.call-start = ((), (), s32[]{:S(2)}) async-start(), calls=%async_computation.2 | async-start | bytes 2621440 | tf_op jit(solution)/shard_map/psum | solution.py:15
  121.5 171.3 %all-reduce.10.cloned.1.call-start = ((), (), s32[]{:S(2)}) async-start(), calls=%async_computation.4 | async-start | bytes 2621440 | tf_op jit(solution)/shard_map/psum | solution.py:15
  207.5 178.7 %all-reduce.12.cloned.1.call-start = ((), (), s32[]{:S(2)}) async-start(), calls=%async_computation.5 | async-start | bytes 2621440 | tf_op jit(solution)/shard_map/psum | solution.py:15
  298.5 180.1 %all-reduce.14.cloned.1.call-start = ((), (), s32[]{:S(2)}) async-start(), calls=%async_computation.6 | async-start | bytes 2621440 | tf_op jit(solution)/shard_map/psum | solution.py:15
  391.5 178.6 %all-reduce.16.cloned.1.call-start = ((), (), s32[]{:S(2)}) async-start(), calls=%async_computation.7 | async-start | bytes 2621440 | tf_op jit(solution)/shard_map/psum | solution.py:15
  484.1 176.4 %all-reduce.18.cloned.1.call-start = ((), (), s32[]{:S(2)}) async-start(), calls=%async_computation.8 | async-start | bytes 2621440 | tf_op jit(solution)/shard_map/psum | solution.py:15
  575.5 177.3 %all-reduce.20.cloned.1.call-start = ((), (), s32[]{:S(2)}) async-start(), calls=%async_computation.9 | async-start | bytes 2621440 | tf_op jit(solution)/shard_map/psum | solution.py:15
Sparse Core Ops, SparseCore 0:
  10.7 112.1 all-gather.1
Sparse Core Ops, SparseCore 1:
  121.6 80.6 all-reduce.7
  207.6 85.1 all-reduce.9
  298.6 87.6 all-reduce.11
  391.6 86.9 all-reduce.13
  484.2 86.0 all-reduce.15
  575.6 84.9 all-reduce.17
  665.9 86.8 all-reduce.19
